TPU v7x, 512 devices: a whole 4x8x8 slice. The times are simulated.
512 devices in a mesh: row: 64 (over x, y, core), col: 8 (over z).
Axes of the slice: x: 4, y: 8, z: 8, core: 2. Of those that a mesh axis runs over, the one named last changes fastest.
Arguments:
- matrix: float32 [16384, 4096], P('row', 'col'), may hold values from -7.8125 to 7.8125
Outputs:
- r_top: float32 [512, 4096], P(None, 'col')
- basis: float32 [16384, 512], P('row')
All inputs are finite; a program needn't handle non-finite values.
Results may differ from a plain program's by a relative error of at most 0.0003.
Values sent between devices are 32-bit elements; how exact they have to be, the bound alone decides.
No kernel may reach another device: no remote copies, remote signals or barrier semaphores. Data moves between devices by JAX's collectives and lax.ppermute only.
A program may use at most 64 MiB of HBM per device.

v0:
```python
import math

import jax
import jax.numpy as jnp
from jax import lax
from jax.experimental import pallas as pl
from jax.experimental.pallas import tpu as pltpu
from jax.sharding import Mesh
from jax.sharding import PartitionSpec as P


PANEL = 256
WIDE = 2 * PANEL
TILE = 128
STEP = 32
ROW = ("x", "y", "core")
PLANE = ("x", "y")
HIGHEST = lax.Precision.HIGHEST


def inner(left, right):
    return lax.dot_general(
        left,
        right,
        (((0,), (0,)), ((), ())),
        precision=HIGHEST,
        preferred_element_type=jnp.float32,
    )


def product(left, right):
    return jnp.dot(left, right, precision=HIGHEST, preferred_element_type=jnp.float32)


SLOTS = 3
PLACES = {
    (i, j): (n // SLOTS, n % SLOTS)
    for n, (i, j) in enumerate((i, j) for i in range(4) for j in range(i, 4))
}


def blocks_of(place):
    return tuple(slice(p * TILE, (p + 1) * TILE) for p in place)


def gram_kernel(panels_ref, out_ref):
    for i in range(4):
        left = panels_ref[:, i * TILE : (i + 1) * TILE]
        line = inner(left, panels_ref[:, i * TILE :])
        for j in range(i, 4):
            out_ref[blocks_of(PLACES[i, j])] = line[:, (j - i) * TILE : (j - i + 1) * TILE]
    for n in range(len(PLACES), 4 * SLOTS):
        out_ref[blocks_of((n // SLOTS, n % SLOTS))] = jnp.zeros((TILE, TILE), jnp.float32)


def packed_gram(panels):
    vmem = pl.BlockSpec(memory_space=pltpu.VMEM)
    return pl.pallas_call(
        gram_kernel,
        out_shape=jax.ShapeDtypeStruct((WIDE, SLOTS * TILE), jnp.float32),
        in_specs=[vmem],
        out_specs=vmem,
        compiler_params=pltpu.CompilerParams(vmem_limit_bytes=16 * 2**20),
        cost_estimate=pl.CostEstimate(flops=600_000_000, bytes_accessed=2**20, transcendentals=0),
    )(panels)


def factor_kernel(core_ref, own_ref, other_ref, out_ref):
    row8 = lax.broadcasted_iota(jnp.int32, (8, TILE), 0)
    lane = lax.broadcasted_iota(jnp.int32, (8, TILE), 1)
    tiles, groups = WIDE // TILE, STEP // 8
    for half in range(2):

        def take(ref):
            for (i, j), (r, c) in PLACES.items():
                if r // 2 == half:
                    out_ref[blocks_of((i, j))] = ref[blocks_of((r % 2, c))]

        @pl.when(core_ref[0] == half)
        def _():
            take(own_ref)

        @pl.when(core_ref[0] != half)
        def _():
            take(other_ref)

    def outer(t, _):
        base = pl.multiple_of(t * TILE, TILE)
        for u in range(TILE // STEP):
            first = pl.multiple_of(base + u * STEP, STEP)
            block = out_ref[pl.ds(first, STEP), pl.ds(base, TILE)]
            cols = []
            for q in range(STEP):
                spread = jnp.broadcast_to(block[:, u * STEP + q : u * STEP + q + 1], (STEP, TILE))
                cols.append([spread[8 * v : 8 * v + 8] for v in range(groups)])
            rows = []
            for v in range(groups):
                rows.append([])
                for w in range(tiles):
                    values = out_ref[pl.ds(first + 8 * v, 8), TILE * w : TILE * (w + 1)]
                    here = (lane >= u * STEP) & (lane < (u + 1) * STEP) & (t == w)
                    unit = jnp.where(lane - u * STEP == row8 + 8 * v, 1.0, 0.0)
                    rows[v].append(jnp.where(here, unit, values))
            pivots = [None] * groups
            for k in range(STEP):
                vk, sk = k // 8, k % 8
                pivot = jnp.broadcast_to(cols[k][vk][sk : sk + 1], (8, TILE))
                inverse = 1.0 / pivot
                pivots[vk] = pivot if sk == 0 else jnp.where(row8 == sk, pivot, pivots[vk])
                scaled = {}
                for v in range(vk, groups):
                    s = cols[k][v] * inverse
                    scaled[v] = jnp.where(row8 > sk, s, 0.0) if v == vk else s
                for j in range(k + 1, STEP):
                    other = jnp.broadcast_to(cols[k][j // 8][j % 8 : j % 8 + 1], (8, TILE))
                    for v in range(j // 8, groups):
                        cols[j][v] = cols[j][v] - scaled[v] * other
                for w in range(tiles):
                    other = jnp.broadcast_to(rows[vk][w][sk : sk + 1], (8, TILE))
                    for v in range(vk, groups):
                        rows[v][w] = rows[v][w] - scaled[v] * other
            for v in range(groups):
                scale = lax.rsqrt(pivots[v])
                for w in range(tiles):
                    out_ref[pl.ds(first + 8 * v, 8), TILE * w : TILE * (w + 1)] = rows[v][w] * scale
            if u < TILE // STEP - 1:
                rest = TILE - (u + 1) * STEP
                done = out_ref[pl.ds(first, STEP), :]
                left = out_ref[pl.ds(first, STEP), pl.ds(base, TILE)][:, (u + 1) * STEP :]
                old = out_ref[pl.ds(first + STEP, rest), :]
                col = lax.broadcasted_iota(jnp.int32, (rest, WIDE), 1)
                old = jnp.where((col >= first) & (col < first + STEP), 0.0, old)
                out_ref[pl.ds(first + STEP, rest), :] = old - inner(left, done)

        done = out_ref[pl.ds(base, TILE), :]
        row = lax.broadcasted_iota(jnp.int32, (TILE, WIDE), 0) + base
        col = lax.broadcasted_iota(jnp.int32, (TILE, WIDE), 1)
        done = jnp.where((col <= row) | (col >= base + TILE), done, 0.0)

        def below(i, _):
            start = pl.multiple_of(i * TILE, TILE)
            old = out_ref[pl.ds(start, TILE), :]
            old = jnp.where((col >= base) & (col < base + TILE), 0.0, old)
            out_ref[pl.ds(start, TILE), :] = old - inner(
                out_ref[pl.ds(base, TILE), pl.ds(start, TILE)], done
            )
            return 0

        lax.fori_loop(t + 1, tiles, below, 0)
        return 0

    lax.fori_loop(0, tiles, outer, 0)
    row = lax.broadcasted_iota(jnp.int32, (WIDE, WIDE), 0)
    col = lax.broadcasted_iota(jnp.int32, (WIDE, WIDE), 1)
    out_ref[...] = jnp.where(col <= row, out_ref[...], 0.0)


def inverse_factor(core, own, other):
    vmem = pl.BlockSpec(memory_space=pltpu.VMEM)
    return pl.pallas_call(
        factor_kernel,
        out_shape=jax.ShapeDtypeStruct((WIDE, WIDE), jnp.float32),
        in_specs=[pl.BlockSpec(memory_space=pltpu.SMEM), vmem, vmem],
        out_specs=vmem,
        compiler_params=pltpu.CompilerParams(vmem_limit_bytes=16 * 2**20),
        cost_estimate=pl.CostEstimate(
            flops=2_000_000_000, bytes_accessed=2**21, transcendentals=0
        ),
    )(core.reshape(1), own, other)


def exchange(blocks, axis):
    return lax.all_to_all(blocks, axis, 0, 0, tiled=True)


def spread(array, count):
    return jnp.broadcast_to(array[None], (count, *array.shape))


def swapped(array):
    return lax.ppermute(array, "core", [(0, 1), (1, 0)])


def among(index, places):
    found = index == places[0]
    for place in places[1:]:
        found = found | (index == place)
    return found


def steps(matrix):
    rows_all = matrix.shape[0] * lax.axis_size(ROW)
    chips = lax.axis_size(PLANE)
    narrow = SLOTS * TILE
    core = lax.axis_index("core")
    col = lax.axis_index("col")

    far = lax.ppermute(matrix, "col", [(0, 4)])
    packed = packed_gram(matrix)
    half = exchange(packed.reshape(2, -1, narrow), "core").sum(axis=0)
    gram_part = exchange(half.reshape(chips, -1, narrow), PLANE)
    panels = jnp.where(col == 0, matrix, far)
    up = lax.ppermute(panels, "col", [(0, 1), (4, 5)])
    down = lax.ppermute(panels, "col", [(0, 7), (4, 3)])
    gram_part, panels = lax.optimization_barrier((gram_part, panels))
    gram_part = exchange(spread(gram_part.sum(axis=0), lax.axis_size("col")), "col")
    panels = jnp.where(among(col, (1, 5)), up, jnp.where(among(col, (3, 7)), down, panels))
    last = lax.ppermute(panels, "col", [(1, 2), (5, 6)])
    gram_part, panels = lax.optimization_barrier((gram_part, panels))
    own = exchange(spread(gram_part[0], chips), PLANE).reshape(-1, narrow)
    panels = jnp.where(among(col, (2, 6)), last, panels)

    products = inner(panels, matrix).reshape(2, -1, WIDE)
    mine = jnp.where(core == 0, products[0], products[1])
    half = mine + swapped(jnp.where(core == 0, products[1], products[0]))
    half, own = lax.optimization_barrier((half, own))
    part = exchange(half.reshape(chips, -1, WIDE), PLANE)
    inverse = inverse_factor(core, own, swapped(own))
    part, inverse = lax.optimization_barrier((part, inverse))
    half = exchange(spread(part.sum(axis=0), chips), PLANE).reshape(-1, WIDE)
    basis = product(panels, inverse.T) * math.sqrt(rows_all)
    half, basis = lax.optimization_barrier((half, basis))
    first, second = inverse[:, :PANEL], inverse[:, PANEL:]
    there = swapped(half)
    top = product(jnp.where(core == 0, first, second), half)
    top = top + product(jnp.where(core == 0, second, first), there)
    row = lax.broadcasted_iota(jnp.int32, (WIDE, WIDE), 0)
    column = lax.broadcasted_iota(jnp.int32, (WIDE, WIDE), 1)
    top = jnp.where((row > column) & (col == 0), 0.0, top)
    return (top, basis)


def solution(mesh):
    finer = Mesh(
        mesh.devices.reshape(4, 8, 2, mesh.shape["col"]), ("x", "y", "core", "col")
    )
    return jax.shard_map(
        steps,
        mesh=finer,
        in_specs=(P(ROW, "col"),),
        out_specs=(P(None, "col"), P(ROW, None)),
        check_vma=False,
    )
```

profile of v0, /device:TPU:1, one launch (start us, length us, event | category | flops | bytes accessed | tf_op | source)
XLA Modules:
  0.0 147.4 jit_solution(12929541790515963814)
XLA Ops:
  0.6 11.5 %collective-permute-start = (f32[256,512]{1,0:T(8,128)}, f32[256,512]{1,0:T(8,128)S(1)}, u32[]{:S(2)}, u32[]{:S(2)}) collective-permute-start(f32[256,512]{1,0:T(8,128)} %panels_ref.1), channel_id=1, source_target_pairs={{0,4},{8,12},{16,20},{24,28},{32,36},{40,44},{48,52},{56,60},{64,6... | collective-permute-start | bytes 1572872 | tf_op jit(solution)/shard_map/ppermute | solution.py:198
  12.1 0.0 copy-start
  12.1 1.1 copy-done
  13.2 0.9 shard_map.30
  14.1 4.9 %all_to_all.30 = f32[2,256,384]{2,1,0:T(8,128)S(1)} all-to-all(f32[2,256,384]{2,1,0:T(8,128)S(1)} %bitcast.12), channel_id=1, replica_groups=mesh['x'=4,'y'=8,'core'=2,'col'=8] {'core'}, dimensions={0} | all-to-all | bytes 1572864 | tf_op jit(solution)/shard_map/all_to_all | solution.py:173
  19.0 0.8 reduce_sum.27
  19.8 0.0 copy-start.1
  19.8 9.8 %all-to-all-start.1 = ((f32[32,8,384]{2,1,0:T(8,128)}), f32[32,8,384]{2,1,0:T(8,128)S(1)}, u32[]{:S(2)}, u32[]{:S(2)}) async-start(f32[32,8,384]{2,1,0:T(8,128)} %bitcast.1), calls=%async_computation.1 | async-start | bytes 786432 | tf_op jit(solution)/shard_map/all_to_all | solution.py:173
  29.6 0.0 collective-permute-done
  29.7 0.0 copy-done.1
  29.7 0.1 broadcast_select_fusion
  29.8 1.3 collective-permute-start.2
  31.1 1.3 collective-permute-start.1
  32.4 9.0 %all-to-all-done.1 = f32[32,8,384]{2,1,0:T(8,128)S(1)} async-done(((f32[32,8,384]{2,1,0:T(8,128)}), f32[32,8,384]{2,1,0:T(8,128)S(1)}, u32[]{:S(2)}, u32[]{:S(2)}) %all-to-all-start.1) | async-done | bytes 393248 | tf_op jit(solution)/shard_map/all_to_all | solution.py:173
  41.5 0.5 collective-permute-done.2
  41.9 1.3 collective-permute-done.1
  43.3 0.1 select_select_fusion
  43.4 0.7 collective-permute-start.3
  44.2 0.6 broadcast_in_dim.24
  44.8 4.1 %all-to-all-start.2 = ((f32[8,8,384]{2,1,0:T(8,128)}), f32[8,8,384]{2,1,0:T(8,128)S(1)}, u32[]{:S(2)}, u32[]{:S(2)}) async-start(f32[8,8,384]{2,1,0:T(8,128)} %broadcast_in_dim.24), calls=%async_computation.2 | async-start | bytes 196608 | tf_op jit(solution)/shard_map/all_to_all | solution.py:173
  48.9 7.6 %all-to-all-done.2 = f32[8,8,384]{2,1,0:T(8,128)S(1)} async-done(((f32[8,8,384]{2,1,0:T(8,128)}), f32[8,8,384]{2,1,0:T(8,128)S(1)}, u32[]{:S(2)}, u32[]{:S(2)}) %all-to-all-start.2) | async-done | bytes 98336 | tf_op jit(solution)/shard_map/all_to_all | solution.py:173
  56.5 0.0 collective-permute-done.3
  56.5 1.1 fusion.11
  57.6 0.1 slice_select_fusion
  57.7 4.9 %collective-permute-start.4 = (f32[256,512]{1,0:T(8,128)S(1)}, f32[256,512]{1,0:T(8,128)S(1)}, u32[]{:S(2)}, u32[]{:S(2)}) collective-permute-start(f32[256,512]{1,0:T(8,128)S(1)} %slice_select_fusion), channel_id=1, source_target_pairs={{0,8},{8,0},{1,9},{9,1},{2,10},{10,2},{3,11},{11,3},{4,12},{12,4},... | collective-permute-start | bytes 1572872 | tf_op jit(solution)/shard_map/ppermute | solution.py:181
  62.6 0.8 broadcast_in_dim.26
  63.4 9.1 %all-to-all-start.3 = ((f32[32,8,384]{2,1,0:T(8,128)}), f32[32,8,384]{2,1,0:T(8,128)S(1)}, u32[]{:S(2)}, u32[]{:S(2)}) async-start(f32[32,8,384]{2,1,0:T(8,128)} %broadcast_in_dim.26), calls=%async_computation.3 | async-start | bytes 786432 | tf_op jit(solution)/shard_map/all_to_all | solution.py:173
  72.4 0.0 collective-permute-done.4
  72.4 0.9 select_add_fusion
  73.4 11.2 %all-to-all-done.3 = f32[32,8,384]{2,1,0:T(8,128)S(1)} async-done(((f32[32,8,384]{2,1,0:T(8,128)}), f32[32,8,384]{2,1,0:T(8,128)S(1)}, u32[]{:S(2)}, u32[]{:S(2)}) %all-to-all-start.3) | async-done | bytes 393248 | tf_op jit(solution)/shard_map/all_to_all | solution.py:173
  84.6 7.4 %all-to-all-start.4 = ((f32[32,8,512]{2,1,0:T(8,128)}), f32[32,8,512]{2,1,0:T(8,128)S(1)}, u32[]{:S(2)}, u32[]{:S(2)}) async-start(f32[32,8,512]{2,1,0:T(8,128)} %bitcast.4), calls=%async_computation.4 | async-start | bytes 1048576 | tf_op jit(solution)/shard_map/all_to_all | solution.py:173
  92.0 3.0 %collective-permute-start.5 = (f32[256,384]{1,0:T(8,128)S(1)}, f32[256,384]{1,0:T(8,128)S(1)}, u32[]{:S(2)}, u32[]{:S(2)}) collective-permute-start(f32[256,384]{1,0:T(8,128)S(1)} %bitcast.13), channel_id=1, source_target_pairs={{0,8},{8,0},{1,9},{9,1},{2,10},{10,2},{3,11},{11,3},{4,12},{12,4},... | collective-permute-start | bytes 1179656 | tf_op jit(solution)/shard_map/ppermute | solution.py:181
  95.0 1.3 collective-permute-done.5.other_ref
  96.3 17.6 %shard_map.31 = f32[512,512]{1,0:T(8,128)S(1)} custom-call(s32[1]{0:T(128)} %bitcast.5.core_ref, f32[256,384]{1,0:T(8,128)S(1)} %bitcast.14, f32[256,384]{1,0:T(8,128)S(1)} %collective-permute-done.5.other_ref), custom_call_target="tpu_custom_call" | custom-call | flops 2000000000 | bytes 2097152 | tf_op jit(solution)/shard_map/pallas_call | solution.py:160
  113.9 0.0 all-to-all-done.4
  113.9 0.9 broadcast_in_dim.27
  114.8 9.5 %all-to-all-start.5 = ((f32[32,8,512]{2,1,0:T(8,128)}), f32[32,8,512]{2,1,0:T(8,128)S(1)}, u32[]{:S(2)}, u32[]{:S(2)}) async-start(f32[32,8,512]{2,1,0:T(8,128)} %broadcast_in_dim.27), calls=%async_computation.5 | async-start | bytes 1048576 | tf_op jit(solution)/shard_map/all_to_all | solution.py:173
  124.3 1.9 %convolution_multiply_fusion = f32[256,512]{1,0:T(8,128)} fusion(f32[512,512]{1,0:T(8,128)S(1)} %shard_map.31, f32[256,512]{1,0:T(8,128)S(1)} %collective-permute-done.3, f32[256,512]{1,0:T(8,128)S(1)} %select_select_fusion, pred[]{:T(512)S(6)} %or.9), kind=kOutput, calls=%fused_computation.2 | convolution fusion | flops 805568512 | bytes 2621441 | tf_op jit(solution)/shard_map/dot_general | solution.py:32
  126.2 12.3 %all-to-all-done.5 = f32[32,8,512]{2,1,0:T(8,128)S(1)} async-done(((f32[32,8,512]{2,1,0:T(8,128)}), f32[32,8,512]{2,1,0:T(8,128)S(1)}, u32[]{:S(2)}, u32[]{:S(2)}) %all-to-all-start.5) | async-done | bytes 524320 | tf_op jit(solution)/shard_map/all_to_all | solution.py:173
  138.5 5.4 %collective-permute-start.6 = (f32[256,512]{1,0:T(8,128)S(1)}, f32[256,512]{1,0:T(8,128)S(1)}, u32[]{:S(2)}, u32[]{:S(2)}) collective-permute-start(f32[256,512]{1,0:T(8,128)S(1)} %bitcast.15), channel_id=1, source_target_pairs={{0,8},{8,0},{1,9},{9,1},{2,10},{10,2},{3,11},{11,3},{4,12},{12,4},... | collective-permute-start | bytes 1572872 | tf_op jit(solution)/shard_map/ppermute | solution.py:181
  143.9 1.0 fusion.3
  144.9 0.5 collective-permute-done.6
  145.4 2.0 %fusion = f32[512,512]{1,0:T(8,128)} fusion(f32[512,512]{1,0:T(8,128)S(1)} %fusion.3, f32[256,512]{1,0:T(8,128)S(1)} %collective-permute-done.6, pred[]{:T(512)S(6)} %eq.28, f32[512,512]{1,0:T(8,128)S(1)} %shard_map.31, pred[]{:T(512)S(6)} %eq.29), kind=kOutput, calls=%fused_computation.1 | convolution fusion | flops 806486016 | bytes 3670018 | tf_op jit(solution)/shard_map/dot_general | solution.py:32
  (3 shorter events, 0.1 us)
Async XLA Ops:
  0.6 29.0 %collective-permute-start = (f32[256,512]{1,0:T(8,128)}, f32[256,512]{1,0:T(8,128)S(1)}, u32[]{:S(2)}, u32[]{:S(2)}) collective-permute-start(f32[256,512]{1,0:T(8,128)} %panels_ref.1), channel_id=1, source_target_pairs={{0,4},{8,12},{16,20},{24,28},{32,36},{40,44},{48,52},{56,60},{64,6... | collective-permute-start | bytes 1572872 | tf_op jit(solution)/shard_map/ppermute | solution.py:198
  12.1 1.1 copy-start
  19.8 9.8 %copy-start.1 = (f32[256,512]{1,0:T(8,128)S(1)}, f32[256,512]{1,0:T(8,128)}, u32[]{:S(2)}) copy-start(f32[256,512]{1,0:T(8,128)} %panels_ref.1) | copy-start | bytes 1572868
  19.8 21.6 %all-to-all-start.1 = ((f32[32,8,384]{2,1,0:T(8,128)}), f32[32,8,384]{2,1,0:T(8,128)S(1)}, u32[]{:S(2)}, u32[]{:S(2)}) async-start(f32[32,8,384]{2,1,0:T(8,128)} %bitcast.1), calls=%async_computation.1 | async-start | bytes 786432 | tf_op jit(solution)/shard_map/all_to_all | solution.py:173
  29.8 12.2 %collective-permute-start.2 = (f32[256,512]{1,0:T(8,128)S(1)}, f32[256,512]{1,0:T(8,128)S(1)}, u32[]{:S(2)}, u32[]{:S(2)}) collective-permute-start(f32[256,512]{1,0:T(8,128)S(1)} %broadcast_select_fusion), channel_id=1, source_target_pairs={{0,7},{4,3},{8,15},{12,11},{16,23},{20,19},{24,31},{28,27},{32,39}... | collective-permute-start | bytes 1572872 | tf_op jit(solution)/shard_map/ppermute | solution.py:204
  31.1 12.2 %collective-permute-start.1 = (f32[256,512]{1,0:T(8,128)S(1)}, f32[256,512]{1,0:T(8,128)S(1)}, u32[]{:S(2)}, u32[]{:S(2)}) collective-permute-start(f32[256,512]{1,0:T(8,128)S(1)} %broadcast_select_fusion), channel_id=1, source_target_pairs={{0,1},{4,5},{8,9},{12,13},{16,17},{20,21},{24,25},{28,29},{32,33},... | collective-permute-start | bytes 1572872 | tf_op jit(solution)/shard_map/ppermute | solution.py:203
  43.4 13.1 %collective-permute-start.3 = (f32[256,512]{1,0:T(8,128)S(1)}, f32[256,512]{1,0:T(8,128)S(1)}, u32[]{:S(2)}, u32[]{:S(2)}) collective-permute-start(f32[256,512]{1,0:T(8,128)S(1)} %select_select_fusion), channel_id=1, source_target_pairs={{1,2},{5,6},{9,10},{13,14},{17,18},{21,22},{25,26},{29,30},{33,34}... | collective-permute-start | bytes 1572872 | tf_op jit(solution)/shard_map/ppermute | solution.py:208
  44.8 11.7 %all-to-all-start.2 = ((f32[8,8,384]{2,1,0:T(8,128)}), f32[8,8,384]{2,1,0:T(8,128)S(1)}, u32[]{:S(2)}, u32[]{:S(2)}) async-start(f32[8,8,384]{2,1,0:T(8,128)} %broadcast_in_dim.24), calls=%async_computation.2 | async-start | bytes 196608 | tf_op jit(solution)/shard_map/all_to_all | solution.py:173
  57.7 14.8 %collective-permute-start.4 = (f32[256,512]{1,0:T(8,128)S(1)}, f32[256,512]{1,0:T(8,128)S(1)}, u32[]{:S(2)}, u32[]{:S(2)}) collective-permute-start(f32[256,512]{1,0:T(8,128)S(1)} %slice_select_fusion), channel_id=1, source_target_pairs={{0,8},{8,0},{1,9},{9,1},{2,10},{10,2},{3,11},{11,3},{4,12},{12,4},... | collective-permute-start | bytes 1572872 | tf_op jit(solution)/shard_map/ppermute | solution.py:181
  63.4 21.2 %all-to-all-start.3 = ((f32[32,8,384]{2,1,0:T(8,128)}), f32[32,8,384]{2,1,0:T(8,128)S(1)}, u32[]{:S(2)}, u32[]{:S(2)}) async-start(f32[32,8,384]{2,1,0:T(8,128)} %broadcast_in_dim.26), calls=%async_computation.3 | async-start | bytes 786432 | tf_op jit(solution)/shard_map/all_to_all | solution.py:173
  84.6 29.3 %all-to-all-start.4 = ((f32[32,8,512]{2,1,0:T(8,128)}), f32[32,8,512]{2,1,0:T(8,128)S(1)}, u32[]{:S(2)}, u32[]{:S(2)}) async-start(f32[32,8,512]{2,1,0:T(8,128)} %bitcast.4), calls=%async_computation.4 | async-start | bytes 1048576 | tf_op jit(solution)/shard_map/all_to_all | solution.py:173
  92.0 4.3 %collective-permute-start.5 = (f32[256,384]{1,0:T(8,128)S(1)}, f32[256,384]{1,0:T(8,128)S(1)}, u32[]{:S(2)}, u32[]{:S(2)}) collective-permute-start(f32[256,384]{1,0:T(8,128)S(1)} %bitcast.13), channel_id=1, source_target_pairs={{0,8},{8,0},{1,9},{9,1},{2,10},{10,2},{3,11},{11,3},{4,12},{12,4},... | collective-permute-start | bytes 1179656 | tf_op jit(solution)/shard_map/ppermute | solution.py:181
  114.8 23.7 %all-to-all-start.5 = ((f32[32,8,512]{2,1,0:T(8,128)}), f32[32,8,512]{2,1,0:T(8,128)S(1)}, u32[]{:S(2)}, u32[]{:S(2)}) async-start(f32[32,8,512]{2,1,0:T(8,128)} %broadcast_in_dim.27), calls=%async_computation.5 | async-start | bytes 1048576 | tf_op jit(solution)/shard_map/all_to_all | solution.py:173
  138.5 6.9 %collective-permute-start.6 = (f32[256,512]{1,0:T(8,128)S(1)}, f32[256,512]{1,0:T(8,128)S(1)}, u32[]{:S(2)}, u32[]{:S(2)}) collective-permute-start(f32[256,512]{1,0:T(8,128)S(1)} %bitcast.15), channel_id=1, source_target_pairs={{0,8},{8,0},{1,9},{9,1},{2,10},{10,2},{3,11},{11,3},{4,12},{12,4},... | collective-permute-start | bytes 1572872 | tf_op jit(solution)/shard_map/ppermute | solution.py:181
where the time goes:
time: 149 us; the launch traced here: 147 us
  starting transfers between devices  67.9 us (46%)
  waiting for transfers between devices  43.8 us (29%)
  Pallas kernels  18.5 us (12%)
  matrix products  5.99 us (4%)
  blocking collectives  4.95 us (3%)
  local copies, waits for them, and re-layouts  3.34 us (2%)
  other arithmetic  2.13 us (1%)
    all_to_all x5, waiting for transfers between devices, exchange(): return lax.all_to_all(blocks, axis, 0, 0, tiled=True)  40.2 us
    all_to_all x5, starting transfers between devices, exchange(): return lax.all_to_all(blocks, axis, 0, 0, tiled=True)  39.9 us
    pallas_call x1, Pallas kernels, inverse_factor(): pl.pallas_call(factor_kernel, out_shape=jax.ShapeDtypeStruct((WIDE, WIDE)...  17.6 us
    ppermute x3, starting transfers between devices, swapped(): return lax.ppermute(array, 'core', [(0, 1), (1, 0)])  13.2 us
    ppermute x1, starting transfers between devices, steps(): far = lax.ppermute(matrix, 'col', [(0, 4)])  11.5 us
    all_to_all x1, blocking collectives, exchange(): return lax.all_to_all(blocks, axis, 0, 0, tiled=True)  4.95 us
    dot_general x3, matrix products, product(): jnp.dot(left, right, precision=HIGHEST, preferred_element_type=jnp.float32)  4.93 us
  transfers between devices with their start and end apart: 12, of which 8 were waited for; matrix products, arithmetic and copies ran while one was open for 4% of the time, Pallas kernels for 13%

commit v1 on v0

--- a/solution.py
+++ b/solution.py
@@ -53,22 +53,7 @@
         out_ref[blocks_of((n // SLOTS, n % SLOTS))] = jnp.zeros((TILE, TILE), jnp.float32)
 
 
-def packed_gram(panels):
-    vmem = pl.BlockSpec(memory_space=pltpu.VMEM)
-    return pl.pallas_call(
-        gram_kernel,
-        out_shape=jax.ShapeDtypeStruct((WIDE, SLOTS * TILE), jnp.float32),
-        in_specs=[vmem],
-        out_specs=vmem,
-        compiler_params=pltpu.CompilerParams(vmem_limit_bytes=16 * 2**20),
-        cost_estimate=pl.CostEstimate(flops=600_000_000, bytes_accessed=2**20, transcendentals=0),
-    )(panels)
-
-
-def factor_kernel(core_ref, own_ref, other_ref, out_ref):
-    row8 = lax.broadcasted_iota(jnp.int32, (8, TILE), 0)
-    lane = lax.broadcasted_iota(jnp.int32, (8, TILE), 1)
-    tiles, groups = WIDE // TILE, STEP // 8
+def start_kernel(core_ref, own_ref, other_ref, out_ref):
     for half in range(2):
 
         def take(ref):
@@ -83,6 +68,22 @@
         @pl.when(core_ref[0] != half)
         def _():
             take(other_ref)
+
+    factor_tiles(out_ref, 0, 2)
+
+
+def finish_kernel(state_ref, out_ref):
+    out_ref[...] = state_ref[...]
+    factor_tiles(out_ref, 2, 4)
+    row = lax.broadcasted_iota(jnp.int32, (WIDE, WIDE), 0)
+    col = lax.broadcasted_iota(jnp.int32, (WIDE, WIDE), 1)
+    out_ref[...] = jnp.where(col <= row, out_ref[...], 0.0)
+
+
+def factor_tiles(out_ref, begin, end):
+    row8 = lax.broadcasted_iota(jnp.int32, (8, TILE), 0)
+    lane = lax.broadcasted_iota(jnp.int32, (8, TILE), 1)
+    tiles, groups = WIDE // TILE, STEP // 8
 
     def outer(t, _):
         base = pl.multiple_of(t * TILE, TILE)
@@ -149,24 +150,19 @@
         lax.fori_loop(t + 1, tiles, below, 0)
         return 0
 
-    lax.fori_loop(0, tiles, outer, 0)
-    row = lax.broadcasted_iota(jnp.int32, (WIDE, WIDE), 0)
-    col = lax.broadcasted_iota(jnp.int32, (WIDE, WIDE), 1)
-    out_ref[...] = jnp.where(col <= row, out_ref[...], 0.0)
-
-
-def inverse_factor(core, own, other):
-    vmem = pl.BlockSpec(memory_space=pltpu.VMEM)
+    lax.fori_loop(begin, end, outer, 0)
+
+
+def call(kernel, operands, rows, columns, flops):
+    vmem, smem = pl.BlockSpec(memory_space=pltpu.VMEM), pl.BlockSpec(memory_space=pltpu.SMEM)
     return pl.pallas_call(
-        factor_kernel,
-        out_shape=jax.ShapeDtypeStruct((WIDE, WIDE), jnp.float32),
-        in_specs=[pl.BlockSpec(memory_space=pltpu.SMEM), vmem, vmem],
+        kernel,
+        out_shape=jax.ShapeDtypeStruct((rows, columns), jnp.float32),
+        in_specs=[smem if a.ndim == 1 else vmem for a in operands],
         out_specs=vmem,
         compiler_params=pltpu.CompilerParams(vmem_limit_bytes=16 * 2**20),
-        cost_estimate=pl.CostEstimate(
-            flops=2_000_000_000, bytes_accessed=2**21, transcendentals=0
-        ),
-    )(core.reshape(1), own, other)
+        cost_estimate=pl.CostEstimate(flops=flops, bytes_accessed=2**21, transcendentals=0),
+    )(*operands)
 
 
 def exchange(blocks, axis):
@@ -179,13 +175,6 @@
 
 def swapped(array):
     return lax.ppermute(array, "core", [(0, 1), (1, 0)])
-
-
-def among(index, places):
-    found = index == places[0]
-    for place in places[1:]:
-        found = found | (index == place)
-    return found
 
 
 def steps(matrix):
@@ -195,29 +184,27 @@
     core = lax.axis_index("core")
     col = lax.axis_index("col")
 
-    far = lax.ppermute(matrix, "col", [(0, 4)])
-    packed = packed_gram(matrix)
+    up = lax.ppermute(matrix, "col", [(0, 3)])
+    down = lax.ppermute(matrix, "col", [(0, 5)])
+    packed = call(gram_kernel, (matrix,), WIDE, narrow, 600_000_000)
     half = exchange(packed.reshape(2, -1, narrow), "core").sum(axis=0)
     gram_part = exchange(half.reshape(chips, -1, narrow), PLANE)
-    panels = jnp.where(col == 0, matrix, far)
-    up = lax.ppermute(panels, "col", [(0, 1), (4, 5)])
-    down = lax.ppermute(panels, "col", [(0, 7), (4, 3)])
+    panels = jnp.where(col == 0, matrix, up + down)
+    up = lax.ppermute(panels, "col", [(0, 1), (3, 4), (5, 6)])
+    down = lax.ppermute(panels, "col", [(0, 7), (3, 2)])
     gram_part, panels = lax.optimization_barrier((gram_part, panels))
     gram_part = exchange(spread(gram_part.sum(axis=0), lax.axis_size("col")), "col")
-    panels = jnp.where(among(col, (1, 5)), up, jnp.where(among(col, (3, 7)), down, panels))
-    last = lax.ppermute(panels, "col", [(1, 2), (5, 6)])
-    gram_part, panels = lax.optimization_barrier((gram_part, panels))
     own = exchange(spread(gram_part[0], chips), PLANE).reshape(-1, narrow)
-    panels = jnp.where(among(col, (2, 6)), last, panels)
-
+    panels = jnp.where((col == 0) | (col == 3) | (col == 5), panels, up + down)
     products = inner(panels, matrix).reshape(2, -1, WIDE)
     mine = jnp.where(core == 0, products[0], products[1])
     half = mine + swapped(jnp.where(core == 0, products[1], products[0]))
     half, own = lax.optimization_barrier((half, own))
     part = exchange(half.reshape(chips, -1, WIDE), PLANE)
-    inverse = inverse_factor(core, own, swapped(own))
-    part, inverse = lax.optimization_barrier((part, inverse))
+    state = call(start_kernel, (core.reshape(1), own, swapped(own)), WIDE, WIDE, 1_000_000_000)
+    part, state = lax.optimization_barrier((part, state))
     half = exchange(spread(part.sum(axis=0), chips), PLANE).reshape(-1, WIDE)
+    inverse = call(finish_kernel, (state,), WIDE, WIDE, 1_000_000_000)
     basis = product(panels, inverse.T) * math.sqrt(rows_all)
     half, basis = lax.optimization_barrier((half, basis))
     first, second = inverse[:, :PANEL], inverse[:, PANEL:]

time: 149 us -> 131 us (0.88)
  waiting for transfers between devices: 43.8 us -> 25.3 us
    all_to_all x5, waiting for transfers between devices: 40.2 us -> 23.4 us  [exchange(): return lax.all_to_all(blocks, axis, 0, 0, tiled=True)]
    all_to_all x5, starting transfers between devices: 39.9 us -> 37.5 us  [exchange(): return lax.all_to_all(blocks, axis, 0, 0, tiled=True)]
    ppermute x3, starting transfers between devices: 13.2 us -> 15.5 us  [swapped(): return lax.ppermute(array, 'core', [(0, 1), (1, 0)])]
    ppermute x4, waiting for transfers between devices: 1.81 us -> 0.01 us  [the longest x1 0.01 us: steps(): down = lax.ppermute(matrix, 'col', [(0, 5)])]
    pallas_call x2 -> x3, Pallas kernels: 18.5 us -> 18.5 us  [call(): pl.pallas_call(kernel, out_shape=jax.ShapeDtypeStruct((rows, columns), jn...]
  transfers between devices with their start and end apart: 12 -> 12, of which waited for: 8 -> 6; matrix products, arithmetic and copies ran while one was open for 4% -> 6% of each run, Pallas kernels for 13% -> 14%
where the time goes in v1:
time: 131 us; the launch traced here: 130 us
  starting transfers between devices  68.5 us (52%)
  waiting for transfers between devices  25.3 us (19%)
  Pallas kernels  18.5 us (14%)
  matrix products  5.94 us (5%)
  blocking collectives  4.95 us (4%)
  local copies, waits for them, and re-layouts  3.34 us (3%)
  other arithmetic  2.2 us (2%)
    all_to_all x5, starting transfers between devices, exchange(): return lax.all_to_all(blocks, axis, 0, 0, tiled=True)  37.5 us
    all_to_all x5, waiting for transfers between devices, exchange(): return lax.all_to_all(blocks, axis, 0, 0, tiled=True)  23.4 us
    pallas_call x3, Pallas kernels, call(): pl.pallas_call(kernel, out_shape=jax.ShapeDtypeStruct((rows, columns), jn...  18.5 us
    ppermute x3, starting transfers between devices, swapped(): return lax.ppermute(array, 'core', [(0, 1), (1, 0)])  15.5 us
    ppermute x1, starting transfers between devices, steps(): down = lax.ppermute(matrix, 'col', [(0, 5)])  11.5 us
    all_to_all x1, blocking collectives, exchange(): return lax.all_to_all(blocks, axis, 0, 0, tiled=True)  4.95 us
    dot_general x3, matrix products, product(): jnp.dot(left, right, precision=HIGHEST, preferred_element_type=jnp.float32)  4.91 us
  transfers between devices with their start and end apart: 12, of which 6 were waited for; matrix products, arithmetic and copies ran while one was open for 6% of the time, Pallas kernels for 14%

profile of v1, /device:TPU:1, one launch (start us, length us, event | category | flops | bytes accessed | tf_op | source)
XLA Modules:
  0.0 129.6 jit_solution(2871690990161720004)
XLA Ops:
  0.6 11.5 %collective-permute-start.1 = (f32[256,512]{1,0:T(8,128)}, f32[256,512]{1,0:T(8,128)S(1)}, u32[]{:S(2)}, u32[]{:S(2)}) collective-permute-start(f32[256,512]{1,0:T(8,128)} %panels_ref.1), channel_id=1, source_target_pairs={{0,5},{8,13},{16,21},{24,29},{32,37},{40,45},{48,53},{56,61},{64,6... | collective-permute-start | bytes 1572872 | tf_op jit(solution)/shard_map/ppermute | solution.py:188
  12.1 1.3 %collective-permute-start = (f32[256,512]{1,0:T(8,128)}, f32[256,512]{1,0:T(8,128)S(1)}, u32[]{:S(2)}, u32[]{:S(2)}) collective-permute-start(f32[256,512]{1,0:T(8,128)} %panels_ref.1), channel_id=1, source_target_pairs={{0,3},{8,11},{16,19},{24,27},{32,35},{40,43},{48,51},{56,59},{64,6... | collective-permute-start | bytes 1572872 | tf_op jit(solution)/shard_map/ppermute | solution.py:187
  13.5 0.0 copy-start
  13.5 1.1 copy-done
  14.5 0.9 shard_map.30
  15.4 4.9 %all_to_all.30 = f32[2,256,384]{2,1,0:T(8,128)S(1)} all-to-all(f32[2,256,384]{2,1,0:T(8,128)S(1)} %bitcast.14), channel_id=1, replica_groups=mesh['x'=4,'y'=8,'core'=2,'col'=8] {'core'}, dimensions={0} | all-to-all | bytes 1572864 | tf_op jit(solution)/shard_map/all_to_all | solution.py:169
  20.4 0.8 reduce_sum.27
  21.2 0.0 copy-start.1
  21.2 9.8 %all-to-all-start.1 = ((f32[32,8,384]{2,1,0:T(8,128)}), f32[32,8,384]{2,1,0:T(8,128)S(1)}, u32[]{:S(2)}, u32[]{:S(2)}) async-start(f32[32,8,384]{2,1,0:T(8,128)} %bitcast.1), calls=%async_computation.1 | async-start | bytes 786432 | tf_op jit(solution)/shard_map/all_to_all | solution.py:169
  31.0 0.0 collective-permute-done.1
  31.0 0.0 collective-permute-done
  31.0 0.0 copy-done.1
  31.0 0.1 add_select_fusion.1
  31.2 1.3 %collective-permute-start.3 = (f32[256,512]{1,0:T(8,128)S(1)}, f32[256,512]{1,0:T(8,128)S(1)}, u32[]{:S(2)}, u32[]{:S(2)}) collective-permute-start(f32[256,512]{1,0:T(8,128)S(1)} %add_select_fusion.1), channel_id=1, source_target_pairs={{0,7},{3,2},{8,15},{11,10},{16,23},{19,18},{24,31},{27,26},{32,39}... | collective-permute-start | bytes 1572872 | tf_op jit(solution)/shard_map/ppermute | solution.py:194
  32.5 1.3 %collective-permute-start.2 = (f32[256,512]{1,0:T(8,128)S(1)}, f32[256,512]{1,0:T(8,128)S(1)}, u32[]{:S(2)}, u32[]{:S(2)}) collective-permute-start(f32[256,512]{1,0:T(8,128)S(1)} %add_select_fusion.1), channel_id=1, source_target_pairs={{0,1},{3,4},{5,6},{8,9},{11,12},{13,14},{16,17},{19,20},{21,22},{2... | collective-permute-start | bytes 1572872 | tf_op jit(solution)/shard_map/ppermute | solution.py:193
  33.9 9.0 %all-to-all-done.1 = f32[32,8,384]{2,1,0:T(8,128)S(1)} async-done(((f32[32,8,384]{2,1,0:T(8,128)}), f32[32,8,384]{2,1,0:T(8,128)S(1)}, u32[]{:S(2)}, u32[]{:S(2)}) %all-to-all-start.1) | async-done | bytes 393248 | tf_op jit(solution)/shard_map/all_to_all | solution.py:169
  42.8 0.6 broadcast_in_dim.24
  43.5 3.4 %all-to-all-start.2 = ((f32[8,8,384]{2,1,0:T(8,128)}), f32[8,8,384]{2,1,0:T(8,128)S(1)}, u32[]{:S(2)}, u32[]{:S(2)}) async-start(f32[8,8,384]{2,1,0:T(8,128)} %broadcast_in_dim.24), calls=%async_computation.2 | async-start | bytes 196608 | tf_op jit(solution)/shard_map/all_to_all | solution.py:169
  46.9 0.0 collective-permute-done.3
  46.9 0.0 collective-permute-done.2
  46.9 0.2 add_select_fusion
  47.0 1.0 fusion.11
  48.1 0.1 slice_select_fusion
  48.2 5.1 %collective-permute-start.4 = (f32[256,512]{1,0:T(8,128)S(1)}, f32[256,512]{1,0:T(8,128)S(1)}, u32[]{:S(2)}, u32[]{:S(2)}) collective-permute-start(f32[256,512]{1,0:T(8,128)S(1)} %slice_select_fusion), channel_id=1, source_target_pairs={{0,8},{8,0},{1,9},{9,1},{2,10},{10,2},{3,11},{11,3},{4,12},{12,4},... | collective-permute-start | bytes 1572872 | tf_op jit(solution)/shard_map/ppermute | solution.py:177
  53.3 1.0 all-to-all-done.2
  54.4 0.8 broadcast_in_dim.26
  55.1 7.4 %all-to-all-start.3 = ((f32[32,8,384]{2,1,0:T(8,128)}), f32[32,8,384]{2,1,0:T(8,128)S(1)}, u32[]{:S(2)}, u32[]{:S(2)}) async-start(f32[32,8,384]{2,1,0:T(8,128)} %broadcast_in_dim.26), calls=%async_computation.3 | async-start | bytes 786432 | tf_op jit(solution)/shard_map/all_to_all | solution.py:169
  62.5 0.0 collective-permute-done.4
  62.5 0.9 select_add_fusion
  63.5 9.3 %all-to-all-done.3 = f32[32,8,384]{2,1,0:T(8,128)S(1)} async-done(((f32[32,8,384]{2,1,0:T(8,128)}), f32[32,8,384]{2,1,0:T(8,128)S(1)}, u32[]{:S(2)}, u32[]{:S(2)}) %all-to-all-start.3) | async-done | bytes 393248 | tf_op jit(solution)/shard_map/all_to_all | solution.py:169
  72.8 7.3 %all-to-all-start.4 = ((f32[32,8,512]{2,1,0:T(8,128)}), f32[32,8,512]{2,1,0:T(8,128)S(1)}, u32[]{:S(2)}, u32[]{:S(2)}) async-start(f32[32,8,512]{2,1,0:T(8,128)} %bitcast.4), calls=%async_computation.4 | async-start | bytes 1048576 | tf_op jit(solution)/shard_map/all_to_all | solution.py:169
  80.1 5.0 %collective-permute-start.5 = (f32[256,384]{1,0:T(8,128)S(1)}, f32[256,384]{1,0:T(8,128)S(1)}, u32[]{:S(2)}, u32[]{:S(2)}) collective-permute-start(f32[256,384]{1,0:T(8,128)S(1)} %bitcast.15), channel_id=1, source_target_pairs={{0,8},{8,0},{1,9},{9,1},{2,10},{10,2},{3,11},{11,3},{4,12},{12,4},... | collective-permute-start | bytes 1179656 | tf_op jit(solution)/shard_map/ppermute | solution.py:177
  85.1 1.3 %collective-permute-done.5.other_ref = f32[256,384]{1,0:T(8,128)S(1)} collective-permute-done((f32[256,384]{1,0:T(8,128)S(1)}, f32[256,384]{1,0:T(8,128)S(1)}, u32[]{:S(2)}, u32[]{:S(2)}) %collective-permute-start.5) | collective-permute-done | bytes 393248 | tf_op jit(solution)/shard_map/ppermute | solution.py:177
  86.4 9.7 %shard_map.31.state_ref = f32[512,512]{1,0:T(8,128)S(1)} custom-call(s32[1]{0:T(128)} %bitcast.5.core_ref, f32[256,384]{1,0:T(8,128)S(1)} %bitcast.16, f32[256,384]{1,0:T(8,128)S(1)} %collective-permute-done.5.other_ref), custom_call_target="tpu_custom_call" | custom-call | flops 1000000000 | bytes 2097152 | tf_op jit(solution)/shard_map/pallas_call | solution.py:158
  96.1 0.0 all-to-all-done.4
  96.1 0.9 broadcast_in_dim.27
  97.0 9.7 %all-to-all-start.5 = ((f32[32,8,512]{2,1,0:T(8,128)}), f32[32,8,512]{2,1,0:T(8,128)S(1)}, u32[]{:S(2)}, u32[]{:S(2)}) async-start(f32[32,8,512]{2,1,0:T(8,128)} %broadcast_in_dim.27), calls=%async_computation.5 | async-start | bytes 1048576 | tf_op jit(solution)/shard_map/all_to_all | solution.py:169
  106.7 8.0 %shard_map.32 = f32[512,512]{1,0:T(8,128)S(1)} custom-call(f32[512,512]{1,0:T(8,128)S(1)} %shard_map.31.state_ref), custom_call_target="tpu_custom_call" | custom-call | flops 1000000000 | bytes 2097152 | tf_op jit(solution)/shard_map/pallas_call | solution.py:158
  114.7 1.9 %convolution_multiply_fusion = f32[256,512]{1,0:T(8,128)} fusion(f32[256,512]{1,0:T(8,128)S(1)} %add_select_fusion, f32[512,512]{1,0:T(8,128)S(1)} %shard_map.32), kind=kOutput, calls=%fused_computation.2 | convolution fusion | flops 805437440 | bytes 2097152 | tf_op jit(solution)/shard_map/dot_general | solution.py:32
  116.5 4.2 %all-to-all-done.5 = f32[32,8,512]{2,1,0:T(8,128)S(1)} async-done(((f32[32,8,512]{2,1,0:T(8,128)}), f32[32,8,512]{2,1,0:T(8,128)S(1)}, u32[]{:S(2)}, u32[]{:S(2)}) %all-to-all-start.5) | async-done | bytes 524320 | tf_op jit(solution)/shard_map/all_to_all | solution.py:169
  120.7 5.4 %collective-permute-start.6 = (f32[256,512]{1,0:T(8,128)S(1)}, f32[256,512]{1,0:T(8,128)S(1)}, u32[]{:S(2)}, u32[]{:S(2)}) collective-permute-start(f32[256,512]{1,0:T(8,128)S(1)} %bitcast.17), channel_id=1, source_target_pairs={{0,8},{8,0},{1,9},{9,1},{2,10},{10,2},{3,11},{11,3},{4,12},{12,4},... | collective-permute-start | bytes 1572872 | tf_op jit(solution)/shard_map/ppermute | solution.py:177
  126.1 1.0 fusion.3
  127.1 0.5 collective-permute-done.6
  127.6 2.0 %fusion = f32[512,512]{1,0:T(8,128)} fusion(f32[512,512]{1,0:T(8,128)S(1)} %fusion.3, f32[256,512]{1,0:T(8,128)S(1)} %collective-permute-done.6, pred[]{:T(512)S(6)} %eq.8, f32[512,512]{1,0:T(8,128)S(1)} %shard_map.32, pred[]{:T(512)S(6)} %eq.18), kind=kOutput, calls=%fused_computation.1 | convolution fusion | flops 806486016 | bytes 3670018 | tf_op jit(solution)/shard_map/dot_general | solution.py:32
  (3 shorter events, 0.1 us)
Async XLA Ops:
  0.6 30.4 %collective-permute-start.1 = (f32[256,512]{1,0:T(8,128)}, f32[256,512]{1,0:T(8,128)S(1)}, u32[]{:S(2)}, u32[]{:S(2)}) collective-permute-start(f32[256,512]{1,0:T(8,128)} %panels_ref.1), channel_id=1, source_target_pairs={{0,5},{8,13},{16,21},{24,29},{32,37},{40,45},{48,53},{56,61},{64,6... | collective-permute-start | bytes 1572872 | tf_op jit(solution)/shard_map/ppermute | solution.py:188
  12.1 18.9 %collective-permute-start = (f32[256,512]{1,0:T(8,128)}, f32[256,512]{1,0:T(8,128)S(1)}, u32[]{:S(2)}, u32[]{:S(2)}) collective-permute-start(f32[256,512]{1,0:T(8,128)} %panels_ref.1), channel_id=1, source_target_pairs={{0,3},{8,11},{16,19},{24,27},{32,35},{40,43},{48,51},{56,59},{64,6... | collective-permute-start | bytes 1572872 | tf_op jit(solution)/shard_map/ppermute | solution.py:187
  13.5 1.1 copy-start
  21.2 9.8 %copy-start.1 = (f32[256,512]{1,0:T(8,128)S(1)}, f32[256,512]{1,0:T(8,128)}, u32[]{:S(2)}) copy-start(f32[256,512]{1,0:T(8,128)} %panels_ref.1) | copy-start | bytes 1572868
  21.2 21.6 %all-to-all-start.1 = ((f32[32,8,384]{2,1,0:T(8,128)}), f32[32,8,384]{2,1,0:T(8,128)S(1)}, u32[]{:S(2)}, u32[]{:S(2)}) async-start(f32[32,8,384]{2,1,0:T(8,128)} %bitcast.1), calls=%async_computation.1 | async-start | bytes 786432 | tf_op jit(solution)/shard_map/all_to_all | solution.py:169
  31.2 15.7 %collective-permute-start.3 = (f32[256,512]{1,0:T(8,128)S(1)}, f32[256,512]{1,0:T(8,128)S(1)}, u32[]{:S(2)}, u32[]{:S(2)}) collective-permute-start(f32[256,512]{1,0:T(8,128)S(1)} %add_select_fusion.1), channel_id=1, source_target_pairs={{0,7},{3,2},{8,15},{11,10},{16,23},{19,18},{24,31},{27,26},{32,39}... | collective-permute-start | bytes 1572872 | tf_op jit(solution)/shard_map/ppermute | solution.py:194
  32.5 14.4 %collective-permute-start.2 = (f32[256,512]{1,0:T(8,128)S(1)}, f32[256,512]{1,0:T(8,128)S(1)}, u32[]{:S(2)}, u32[]{:S(2)}) collective-permute-start(f32[256,512]{1,0:T(8,128)S(1)} %add_select_fusion.1), channel_id=1, source_target_pairs={{0,1},{3,4},{5,6},{8,9},{11,12},{13,14},{16,17},{19,20},{21,22},{2... | collective-permute-start | bytes 1572872 | tf_op jit(solution)/shard_map/ppermute | solution.py:193
  43.5 10.9 %all-to-all-start.2 = ((f32[8,8,384]{2,1,0:T(8,128)}), f32[8,8,384]{2,1,0:T(8,128)S(1)}, u32[]{:S(2)}, u32[]{:S(2)}) async-start(f32[8,8,384]{2,1,0:T(8,128)} %broadcast_in_dim.24), calls=%async_computation.2 | async-start | bytes 196608 | tf_op jit(solution)/shard_map/all_to_all | solution.py:169
  48.2 14.4 %collective-permute-start.4 = (f32[256,512]{1,0:T(8,128)S(1)}, f32[256,512]{1,0:T(8,128)S(1)}, u32[]{:S(2)}, u32[]{:S(2)}) collective-permute-start(f32[256,512]{1,0:T(8,128)S(1)} %slice_select_fusion), channel_id=1, source_target_pairs={{0,8},{8,0},{1,9},{9,1},{2,10},{10,2},{3,11},{11,3},{4,12},{12,4},... | collective-permute-start | bytes 1572872 | tf_op jit(solution)/shard_map/ppermute | solution.py:177
  55.1 17.7 %all-to-all-start.3 = ((f32[32,8,384]{2,1,0:T(8,128)}), f32[32,8,384]{2,1,0:T(8,128)S(1)}, u32[]{:S(2)}, u32[]{:S(2)}) async-start(f32[32,8,384]{2,1,0:T(8,128)} %broadcast_in_dim.26), calls=%async_computation.3 | async-start | bytes 786432 | tf_op jit(solution)/shard_map/all_to_all | solution.py:169
  72.8 23.3 %all-to-all-start.4 = ((f32[32,8,512]{2,1,0:T(8,128)}), f32[32,8,512]{2,1,0:T(8,128)S(1)}, u32[]{:S(2)}, u32[]{:S(2)}) async-start(f32[32,8,512]{2,1,0:T(8,128)} %bitcast.4), calls=%async_computation.4 | async-start | bytes 1048576 | tf_op jit(solution)/shard_map/all_to_all | solution.py:169
  80.1 6.3 %collective-permute-start.5 = (f32[256,384]{1,0:T(8,128)S(1)}, f32[256,384]{1,0:T(8,128)S(1)}, u32[]{:S(2)}, u32[]{:S(2)}) collective-permute-start(f32[256,384]{1,0:T(8,128)S(1)} %bitcast.15), channel_id=1, source_target_pairs={{0,8},{8,0},{1,9},{9,1},{2,10},{10,2},{3,11},{11,3},{4,12},{12,4},... | collective-permute-start | bytes 1179656 | tf_op jit(solution)/shard_map/ppermute | solution.py:177
  97.0 23.7 %all-to-all-start.5 = ((f32[32,8,512]{2,1,0:T(8,128)}), f32[32,8,512]{2,1,0:T(8,128)S(1)}, u32[]{:S(2)}, u32[]{:S(2)}) async-start(f32[32,8,512]{2,1,0:T(8,128)} %broadcast_in_dim.27), calls=%async_computation.5 | async-start | bytes 1048576 | tf_op jit(solution)/shard_map/all_to_all | solution.py:169
  120.7 6.9 %collective-permute-start.6 = (f32[256,512]{1,0:T(8,128)S(1)}, f32[256,512]{1,0:T(8,128)S(1)}, u32[]{:S(2)}, u32[]{:S(2)}) collective-permute-start(f32[256,512]{1,0:T(8,128)S(1)} %bitcast.17), channel_id=1, source_target_pairs={{0,8},{8,0},{1,9},{9,1},{2,10},{10,2},{3,11},{11,3},{4,12},{12,4},... | collective-permute-start | bytes 1572872 | tf_op jit(solution)/shard_map/ppermute | solution.py:177

commit v2 on v1

--- a/solution.py
+++ b/solution.py
@@ -69,12 +69,12 @@
         def _():
             take(other_ref)
 
-    factor_tiles(out_ref, 0, 2)
+    factor_tiles(out_ref, 0, 1)
 
 
 def finish_kernel(state_ref, out_ref):
     out_ref[...] = state_ref[...]
-    factor_tiles(out_ref, 2, 4)
+    factor_tiles(out_ref, 1, 4)
     row = lax.broadcasted_iota(jnp.int32, (WIDE, WIDE), 0)
     col = lax.broadcasted_iota(jnp.int32, (WIDE, WIDE), 1)
     out_ref[...] = jnp.where(col <= row, out_ref[...], 0.0)
@@ -192,10 +192,10 @@
     panels = jnp.where(col == 0, matrix, up + down)
     up = lax.ppermute(panels, "col", [(0, 1), (3, 4), (5, 6)])
     down = lax.ppermute(panels, "col", [(0, 7), (3, 2)])
-    gram_part, panels = lax.optimization_barrier((gram_part, panels))
     gram_part = exchange(spread(gram_part.sum(axis=0), lax.axis_size("col")), "col")
     own = exchange(spread(gram_part[0], chips), PLANE).reshape(-1, narrow)
     panels = jnp.where((col == 0) | (col == 3) | (col == 5), panels, up + down)
+    panels = lax.optimization_barrier(panels)
     products = inner(panels, matrix).reshape(2, -1, WIDE)
     mine = jnp.where(core == 0, products[0], products[1])
     half = mine + swapped(jnp.where(core == 0, products[1], products[0]))

time: 131 us -> 126 us (0.962)
  waiting for transfers between devices: 25.3 us -> 21.7 us
    all_to_all x5, waiting for transfers between devices: 23.4 us -> 19.9 us  [exchange(): return lax.all_to_all(blocks, axis, 0, 0, tiled=True)]
  transfers between devices with their start and end apart: 12 -> 12, of which waited for: 6 -> 6; matrix products, arithmetic and copies ran while one was open for 6% -> 6% of each run, Pallas kernels for 14% -> 15%
where the time goes in v2:
time: 126 us; the launch traced here: 125 us
  starting transfers between devices  67.5 us (54%)
  waiting for transfers between devices  21.7 us (17%)
  Pallas kernels  18.4 us (15%)
  matrix products  5.94 us (5%)
  blocking collectives  4.95 us (4%)
  local copies, waits for them, and re-layouts  3.34 us (3%)
  other arithmetic  2.2 us (2%)
    all_to_all x5, starting transfers between devices, exchange(): return lax.all_to_all(blocks, axis, 0, 0, tiled=True)  36.9 us
    all_to_all x5, waiting for transfers between devices, exchange(): return lax.all_to_all(blocks, axis, 0, 0, tiled=True)  19.9 us
    pallas_call x3, Pallas kernels, call(): pl.pallas_call(kernel, out_shape=jax.ShapeDtypeStruct((rows, columns), jn...  18.4 us
    ppermute x3, starting transfers between devices, swapped(): return lax.ppermute(array, 'core', [(0, 1), (1, 0)])  15.1 us
    ppermute x1, starting transfers between devices, steps(): down = lax.ppermute(matrix, 'col', [(0, 5)])  11.5 us
    all_to_all x1, blocking collectives, exchange(): return lax.all_to_all(blocks, axis, 0, 0, tiled=True)  4.95 us
    dot_general x3, matrix products, product(): jnp.dot(left, right, precision=HIGHEST, preferred_element_type=jnp.float32)  4.91 us
  transfers between devices with their start and end apart: 12, of which 6 were waited for; matrix products, arithmetic and copies ran while one was open for 6% of the time, Pallas kernels for 15%

profile of v2, /device:TPU:1, one launch (start us, length us, event | category | flops | bytes accessed | tf_op | source)
XLA Modules:
  0.0 124.9 jit_solution(16018097233153680704)
XLA Ops:
  0.6 11.5 %collective-permute-start.1 = (f32[256,512]{1,0:T(8,128)}, f32[256,512]{1,0:T(8,128)S(1)}, u32[]{:S(2)}, u32[]{:S(2)}) collective-permute-start(f32[256,512]{1,0:T(8,128)} %panels_ref.1), channel_id=1, source_target_pairs={{0,5},{8,13},{16,21},{24,29},{32,37},{40,45},{48,53},{56,61},{64,6... | collective-permute-start | bytes 1572872 | tf_op jit(solution)/shard_map/ppermute | solution.py:188
  12.1 1.3 %collective-permute-start = (f32[256,512]{1,0:T(8,128)}, f32[256,512]{1,0:T(8,128)S(1)}, u32[]{:S(2)}, u32[]{:S(2)}) collective-permute-start(f32[256,512]{1,0:T(8,128)} %panels_ref.1), channel_id=1, source_target_pairs={{0,3},{8,11},{16,19},{24,27},{32,35},{40,43},{48,51},{56,59},{64,6... | collective-permute-start | bytes 1572872 | tf_op jit(solution)/shard_map/ppermute | solution.py:187
  13.5 0.0 copy-start
  13.5 1.1 copy-done
  14.5 0.9 shard_map.30
  15.4 4.9 %all_to_all.30 = f32[2,256,384]{2,1,0:T(8,128)S(1)} all-to-all(f32[2,256,384]{2,1,0:T(8,128)S(1)} %bitcast.14), channel_id=1, replica_groups=mesh['x'=4,'y'=8,'core'=2,'col'=8] {'core'}, dimensions={0} | all-to-all | bytes 1572864 | tf_op jit(solution)/shard_map/all_to_all | solution.py:169
  20.4 0.8 reduce_sum.27
  21.2 0.0 copy-start.1
  21.2 9.8 %all-to-all-start.1 = ((f32[32,8,384]{2,1,0:T(8,128)}), f32[32,8,384]{2,1,0:T(8,128)S(1)}, u32[]{:S(2)}, u32[]{:S(2)}) async-start(f32[32,8,384]{2,1,0:T(8,128)} %bitcast.1), calls=%async_computation.1 | async-start | bytes 786432 | tf_op jit(solution)/shard_map/all_to_all | solution.py:169
  31.0 0.0 collective-permute-done.1
  31.0 0.0 collective-permute-done
  31.0 0.0 copy-done.1
  31.0 0.1 add_select_fusion.1
  31.2 1.3 %collective-permute-start.3 = (f32[256,512]{1,0:T(8,128)S(1)}, f32[256,512]{1,0:T(8,128)S(1)}, u32[]{:S(2)}, u32[]{:S(2)}) collective-permute-start(f32[256,512]{1,0:T(8,128)S(1)} %add_select_fusion.1), channel_id=1, source_target_pairs={{0,7},{3,2},{8,15},{11,10},{16,23},{19,18},{24,31},{27,26},{32,39}... | collective-permute-start | bytes 1572872 | tf_op jit(solution)/shard_map/ppermute | solution.py:194
  32.5 1.3 %collective-permute-start.2 = (f32[256,512]{1,0:T(8,128)S(1)}, f32[256,512]{1,0:T(8,128)S(1)}, u32[]{:S(2)}, u32[]{:S(2)}) collective-permute-start(f32[256,512]{1,0:T(8,128)S(1)} %add_select_fusion.1), channel_id=1, source_target_pairs={{0,1},{3,4},{5,6},{8,9},{11,12},{13,14},{16,17},{19,20},{21,22},{2... | collective-permute-start | bytes 1572872 | tf_op jit(solution)/shard_map/ppermute | solution.py:193
  33.9 9.0 %all-to-all-done.1 = f32[32,8,384]{2,1,0:T(8,128)S(1)} async-done(((f32[32,8,384]{2,1,0:T(8,128)}), f32[32,8,384]{2,1,0:T(8,128)S(1)}, u32[]{:S(2)}, u32[]{:S(2)}) %all-to-all-start.1) | async-done | bytes 393248 | tf_op jit(solution)/shard_map/all_to_all | solution.py:169
  42.8 0.6 broadcast_in_dim.24
  43.5 3.4 %all-to-all-start.2 = ((f32[8,8,384]{2,1,0:T(8,128)}), f32[8,8,384]{2,1,0:T(8,128)S(1)}, u32[]{:S(2)}, u32[]{:S(2)}) async-start(f32[8,8,384]{2,1,0:T(8,128)} %broadcast_in_dim.24), calls=%async_computation.2 | async-start | bytes 196608 | tf_op jit(solution)/shard_map/all_to_all | solution.py:169
  46.9 0.0 collective-permute-done.3
  46.9 0.0 collective-permute-done.2
  46.9 0.2 add_select_fusion
  47.0 1.0 fusion.11
  48.1 0.1 slice_select_fusion
  48.2 5.1 %collective-permute-start.4 = (f32[256,512]{1,0:T(8,128)S(1)}, f32[256,512]{1,0:T(8,128)S(1)}, u32[]{:S(2)}, u32[]{:S(2)}) collective-permute-start(f32[256,512]{1,0:T(8,128)S(1)} %slice_select_fusion), channel_id=1, source_target_pairs={{0,8},{8,0},{1,9},{9,1},{2,10},{10,2},{3,11},{11,3},{4,12},{12,4},... | collective-permute-start | bytes 1572872 | tf_op jit(solution)/shard_map/ppermute | solution.py:177
  53.3 1.0 all-to-all-done.2
  54.4 0.8 broadcast_in_dim.26
  55.1 7.4 %all-to-all-start.3 = ((f32[32,8,384]{2,1,0:T(8,128)}), f32[32,8,384]{2,1,0:T(8,128)S(1)}, u32[]{:S(2)}, u32[]{:S(2)}) async-start(f32[32,8,384]{2,1,0:T(8,128)} %broadcast_in_dim.26), calls=%async_computation.3 | async-start | bytes 786432 | tf_op jit(solution)/shard_map/all_to_all | solution.py:169
  62.5 0.0 collective-permute-done.4
  62.5 0.9 select_add_fusion
  63.5 9.3 %all-to-all-done.3 = f32[32,8,384]{2,1,0:T(8,128)S(1)} async-done(((f32[32,8,384]{2,1,0:T(8,128)}), f32[32,8,384]{2,1,0:T(8,128)S(1)}, u32[]{:S(2)}, u32[]{:S(2)}) %all-to-all-start.3) | async-done | bytes 393248 | tf_op jit(solution)/shard_map/all_to_all | solution.py:169
  72.8 7.3 %all-to-all-start.4 = ((f32[32,8,512]{2,1,0:T(8,128)}), f32[32,8,512]{2,1,0:T(8,128)S(1)}, u32[]{:S(2)}, u32[]{:S(2)}) async-start(f32[32,8,512]{2,1,0:T(8,128)} %bitcast.4), calls=%async_computation.4 | async-start | bytes 1048576 | tf_op jit(solution)/shard_map/all_to_all | solution.py:169
  80.1 5.0 %collective-permute-start.5 = (f32[256,384]{1,0:T(8,128)S(1)}, f32[256,384]{1,0:T(8,128)S(1)}, u32[]{:S(2)}, u32[]{:S(2)}) collective-permute-start(f32[256,384]{1,0:T(8,128)S(1)} %bitcast.15), channel_id=1, source_target_pairs={{0,8},{8,0},{1,9},{9,1},{2,10},{10,2},{3,11},{11,3},{4,12},{12,4},... | collective-permute-start | bytes 1179656 | tf_op jit(solution)/shard_map/ppermute | solution.py:177
  85.1 1.3 %collective-permute-done.5.other_ref = f32[256,384]{1,0:T(8,128)S(1)} collective-permute-done((f32[256,384]{1,0:T(8,128)S(1)}, f32[256,384]{1,0:T(8,128)S(1)}, u32[]{:S(2)}, u32[]{:S(2)}) %collective-permute-start.5) | collective-permute-done | bytes 393248 | tf_op jit(solution)/shard_map/ppermute | solution.py:177
  86.4 4.9 %shard_map.31.state_ref = f32[512,512]{1,0:T(8,128)S(1)} custom-call(s32[1]{0:T(128)} %bitcast.5.core_ref, f32[256,384]{1,0:T(8,128)S(1)} %bitcast.16, f32[256,384]{1,0:T(8,128)S(1)} %collective-permute-done.5.other_ref), custom_call_target="tpu_custom_call" | custom-call | flops 1000000000 | bytes 2097152 | tf_op jit(solution)/shard_map/pallas_call | solution.py:158
  91.4 0.6 all-to-all-done.4
  92.0 0.9 broadcast_in_dim.27
  92.9 9.1 %all-to-all-start.5 = ((f32[32,8,512]{2,1,0:T(8,128)}), f32[32,8,512]{2,1,0:T(8,128)S(1)}, u32[]{:S(2)}, u32[]{:S(2)}) async-start(f32[32,8,512]{2,1,0:T(8,128)} %broadcast_in_dim.27), calls=%async_computation.5 | async-start | bytes 1048576 | tf_op jit(solution)/shard_map/all_to_all | solution.py:169
  102.0 12.6 %shard_map.32 = f32[512,512]{1,0:T(8,128)S(1)} custom-call(f32[512,512]{1,0:T(8,128)S(1)} %shard_map.31.state_ref), custom_call_target="tpu_custom_call" | custom-call | flops 1000000000 | bytes 2097152 | tf_op jit(solution)/shard_map/pallas_call | solution.py:158
  114.5 1.9 %convolution_multiply_fusion = f32[256,512]{1,0:T(8,128)} fusion(f32[256,512]{1,0:T(8,128)S(1)} %add_select_fusion, f32[512,512]{1,0:T(8,128)S(1)} %shard_map.32), kind=kOutput, calls=%fused_computation.2 | convolution fusion | flops 805437440 | bytes 2097152 | tf_op jit(solution)/shard_map/dot_general | solution.py:32
  116.4 0.0 all-to-all-done.5
  116.4 4.9 %collective-permute-start.6 = (f32[256,512]{1,0:T(8,128)S(1)}, f32[256,512]{1,0:T(8,128)S(1)}, u32[]{:S(2)}, u32[]{:S(2)}) collective-permute-start(f32[256,512]{1,0:T(8,128)S(1)} %bitcast.17), channel_id=1, source_target_pairs={{0,8},{8,0},{1,9},{9,1},{2,10},{10,2},{3,11},{11,3},{4,12},{12,4},... | collective-permute-start | bytes 1572872 | tf_op jit(solution)/shard_map/ppermute | solution.py:177
  121.3 1.0 fusion.3
  122.4 0.5 collective-permute-done.6
  122.8 2.0 %fusion = f32[512,512]{1,0:T(8,128)} fusion(f32[512,512]{1,0:T(8,128)S(1)} %fusion.3, f32[256,512]{1,0:T(8,128)S(1)} %collective-permute-done.6, pred[]{:T(512)S(6)} %eq.8, f32[512,512]{1,0:T(8,128)S(1)} %shard_map.32, pred[]{:T(512)S(6)} %eq.18), kind=kOutput, calls=%fused_computation.1 | convolution fusion | flops 806486016 | bytes 3670018 | tf_op jit(solution)/shard_map/dot_general | solution.py:32
  (3 shorter events, 0.1 us)
Async XLA Ops:
  0.6 30.4 %collective-permute-start.1 = (f32[256,512]{1,0:T(8,128)}, f32[256,512]{1,0:T(8,128)S(1)}, u32[]{:S(2)}, u32[]{:S(2)}) collective-permute-start(f32[256,512]{1,0:T(8,128)} %panels_ref.1), channel_id=1, source_target_pairs={{0,5},{8,13},{16,21},{24,29},{32,37},{40,45},{48,53},{56,61},{64,6... | collective-permute-start | bytes 1572872 | tf_op jit(solution)/shard_map/ppermute | solution.py:188
  12.1 18.9 %collective-permute-start = (f32[256,512]{1,0:T(8,128)}, f32[256,512]{1,0:T(8,128)S(1)}, u32[]{:S(2)}, u32[]{:S(2)}) collective-permute-start(f32[256,512]{1,0:T(8,128)} %panels_ref.1), channel_id=1, source_target_pairs={{0,3},{8,11},{16,19},{24,27},{32,35},{40,43},{48,51},{56,59},{64,6... | collective-permute-start | bytes 1572872 | tf_op jit(solution)/shard_map/ppermute | solution.py:187
  13.5 1.1 copy-start
  21.2 9.8 %copy-start.1 = (f32[256,512]{1,0:T(8,128)S(1)}, f32[256,512]{1,0:T(8,128)}, u32[]{:S(2)}) copy-start(f32[256,512]{1,0:T(8,128)} %panels_ref.1) | copy-start | bytes 1572868
  21.2 21.6 %all-to-all-start.1 = ((f32[32,8,384]{2,1,0:T(8,128)}), f32[32,8,384]{2,1,0:T(8,128)S(1)}, u32[]{:S(2)}, u32[]{:S(2)}) async-start(f32[32,8,384]{2,1,0:T(8,128)} %bitcast.1), calls=%async_computation.1 | async-start | bytes 786432 | tf_op jit(solution)/shard_map/all_to_all | solution.py:169
  31.2 15.7 %collective-permute-start.3 = (f32[256,512]{1,0:T(8,128)S(1)}, f32[256,512]{1,0:T(8,128)S(1)}, u32[]{:S(2)}, u32[]{:S(2)}) collective-permute-start(f32[256,512]{1,0:T(8,128)S(1)} %add_select_fusion.1), channel_id=1, source_target_pairs={{0,7},{3,2},{8,15},{11,10},{16,23},{19,18},{24,31},{27,26},{32,39}... | collective-permute-start | bytes 1572872 | tf_op jit(solution)/shard_map/ppermute | solution.py:194
  32.5 14.4 %collective-permute-start.2 = (f32[256,512]{1,0:T(8,128)S(1)}, f32[256,512]{1,0:T(8,128)S(1)}, u32[]{:S(2)}, u32[]{:S(2)}) collective-permute-start(f32[256,512]{1,0:T(8,128)S(1)} %add_select_fusion.1), channel_id=1, source_target_pairs={{0,1},{3,4},{5,6},{8,9},{11,12},{13,14},{16,17},{19,20},{21,22},{2... | collective-permute-start | bytes 1572872 | tf_op jit(solution)/shard_map/ppermute | solution.py:193
  43.5 10.9 %all-to-all-start.2 = ((f32[8,8,384]{2,1,0:T(8,128)}), f32[8,8,384]{2,1,0:T(8,128)S(1)}, u32[]{:S(2)}, u32[]{:S(2)}) async-start(f32[8,8,384]{2,1,0:T(8,128)} %broadcast_in_dim.24), calls=%async_computation.2 | async-start | bytes 196608 | tf_op jit(solution)/shard_map/all_to_all | solution.py:169
  48.2 14.4 %collective-permute-start.4 = (f32[256,512]{1,0:T(8,128)S(1)}, f32[256,512]{1,0:T(8,128)S(1)}, u32[]{:S(2)}, u32[]{:S(2)}) collective-permute-start(f32[256,512]{1,0:T(8,128)S(1)} %slice_select_fusion), channel_id=1, source_target_pairs={{0,8},{8,0},{1,9},{9,1},{2,10},{10,2},{3,11},{11,3},{4,12},{12,4},... | collective-permute-start | bytes 1572872 | tf_op jit(solution)/shard_map/ppermute | solution.py:177
  55.1 17.7 %all-to-all-start.3 = ((f32[32,8,384]{2,1,0:T(8,128)}), f32[32,8,384]{2,1,0:T(8,128)S(1)}, u32[]{:S(2)}, u32[]{:S(2)}) async-start(f32[32,8,384]{2,1,0:T(8,128)} %broadcast_in_dim.26), calls=%async_computation.3 | async-start | bytes 786432 | tf_op jit(solution)/shard_map/all_to_all | solution.py:169
  72.8 19.2 %all-to-all-start.4 = ((f32[32,8,512]{2,1,0:T(8,128)}), f32[32,8,512]{2,1,0:T(8,128)S(1)}, u32[]{:S(2)}, u32[]{:S(2)}) async-start(f32[32,8,512]{2,1,0:T(8,128)} %bitcast.4), calls=%async_computation.4 | async-start | bytes 1048576 | tf_op jit(solution)/shard_map/all_to_all | solution.py:169
  80.1 6.3 %collective-permute-start.5 = (f32[256,384]{1,0:T(8,128)S(1)}, f32[256,384]{1,0:T(8,128)S(1)}, u32[]{:S(2)}, u32[]{:S(2)}) collective-permute-start(f32[256,384]{1,0:T(8,128)S(1)} %bitcast.15), channel_id=1, source_target_pairs={{0,8},{8,0},{1,9},{9,1},{2,10},{10,2},{3,11},{11,3},{4,12},{12,4},... | collective-permute-start | bytes 1179656 | tf_op jit(solution)/shard_map/ppermute | solution.py:177
  92.9 23.5 %all-to-all-start.5 = ((f32[32,8,512]{2,1,0:T(8,128)}), f32[32,8,512]{2,1,0:T(8,128)S(1)}, u32[]{:S(2)}, u32[]{:S(2)}) async-start(f32[32,8,512]{2,1,0:T(8,128)} %broadcast_in_dim.27), calls=%async_computation.5 | async-start | bytes 1048576 | tf_op jit(solution)/shard_map/all_to_all | solution.py:169
  116.4 6.5 %collective-permute-start.6 = (f32[256,512]{1,0:T(8,128)S(1)}, f32[256,512]{1,0:T(8,128)S(1)}, u32[]{:S(2)}, u32[]{:S(2)}) collective-permute-start(f32[256,512]{1,0:T(8,128)S(1)} %bitcast.17), channel_id=1, source_target_pairs={{0,8},{8,0},{1,9},{9,1},{2,10},{10,2},{3,11},{11,3},{4,12},{12,4},... | collective-permute-start | bytes 1572872 | tf_op jit(solution)/shard_map/ppermute | solution.py:177
